TPU v7x, 32 devices: a whole 2x2x4 slice. The times are simulated.
32 devices in a mesh: seq: 8 (over y, x, core), wshard: 4 (over z).
Axes of the slice: x: 2, y: 2, z: 4, core: 2. Of those that a mesh axis runs over, the one named last changes fastest.
Arguments:
- block_in: bfloat16 [4, 2048, 1536], P('wshard', 'seq'), may hold values from -6 to 6
- cotangent: bfloat16 [4, 2048, 1536], P('wshard', 'seq'), may hold values from -6 to 6
- in_weight: float32 [1536, 6448], P(('seq', 'wshard')), may hold values from -0.15625 to 0.15625
- out_weight: float32 [3072, 1536], P(('seq', 'wshard')), may hold values from -0.109375 to 0.109375
- in_gain: float32 [1536], replicated, may hold values from 0.5 to 1.5
- out_gain: float32 [3072], replicated, may hold values from 0.5 to 1.5
- conv_inner: float32 [5, 3072], replicated, may hold values from -3 to 3
- conv_shared: float32 [5, 256], replicated, may hold values from -3 to 3
- head_params: float32 [3, 48], replicated, may hold values from -5 to 1.5, as said below
- first_in_weight: float32 [1536, 6448], P(('seq', 'wshard')), may hold values from -6 to 6
- first_out_weight: float32 [3072, 1536], P(('seq', 'wshard')), may hold values from -6 to 6
- first_in_gain: float32 [1536], replicated, may hold values from -6 to 6
- first_out_gain: float32 [3072], replicated, may hold values from -6 to 6
- first_conv_inner: float32 [5, 3072], replicated, may hold values from -6 to 6
- first_conv_shared: float32 [5, 256], replicated, may hold values from -6 to 6
- first_head_params: float32 [3, 48], replicated, may hold values from -6 to 6
- second_in_weight: float32 [1536, 6448], P(('seq', 'wshard')), may hold values from 0.01 to 1
- second_out_weight: float32 [3072, 1536], P(('seq', 'wshard')), may hold values from 0.01 to 1
- second_in_gain: float32 [1536], replicated, may hold values from 16.384 to 1638.4
- second_out_gain: float32 [3072], replicated, may hold values from 0.01 to 1
- second_conv_inner: float32 [5, 3072], replicated, may hold values from 0.01 to 1
- second_conv_shared: float32 [5, 256], replicated, may hold values from 0.01 to 1
- second_head_params: float32 [3, 48], replicated, may hold values from 0.01 to 1
Outputs:
- block_out: float32 [4, 2048, 1536], P('wshard', 'seq')
- grad_in: float32 [4, 2048, 1536], P('wshard', 'seq')
- grad_in_weight: float32 [1536, 6448], P(('seq', 'wshard'))
- grad_out_weight: float32 [3072, 1536], P(('seq', 'wshard'))
- grad_in_gain: float32 [1536], replicated
- grad_out_gain: float32 [3072], replicated
- grad_conv_inner: float32 [5, 3072], replicated
- grad_conv_shared: float32 [5, 256], replicated
- grad_head_params: float32 [3, 48], replicated
- new_in_weight: float32 [1536, 6448], P(('seq', 'wshard'))
- new_out_weight: float32 [3072, 1536], P(('seq', 'wshard'))
- updated_input_gain: float32 [1536], replicated
- new_out_gain: float32 [3072], replicated
- new_conv_inner: float32 [5, 3072], replicated
- new_conv_shared: float32 [5, 256], replicated
- new_head_params: float32 [3, 48], replicated
- new_first_in_weight: float32 [1536, 6448], P(('seq', 'wshard'))
- new_first_out_weight: float32 [3072, 1536], P(('seq', 'wshard'))
- new_first_in_gain: float32 [1536], replicated
- new_first_out_gain: float32 [3072], replicated
- new_first_conv_inner: float32 [5, 3072], replicated
- new_first_conv_shared: float32 [5, 256], replicated
- updated_head_first_moment: float32 [3, 48], replicated
- new_second_in_weight: float32 [1536, 6448], P(('seq', 'wshard'))
- new_second_out_weight: float32 [3072, 1536], P(('seq', 'wshard'))
- new_second_in_gain: float32 [1536], replicated
- new_second_out_gain: float32 [3072], replicated
- new_second_conv_inner: float32 [5, 3072], replicated
- new_second_conv_shared: float32 [5, 256], replicated
- new_second_head_params: float32 [2, 48], replicated
- new_second_skip: float32 [48], replicated
Inputs may be any that keep to these rules, and one draw needn't show every extreme that they name: `head_params`: row 0 holds step biases, row 1 logarithms of decay rates, row 2 skip gains.
All inputs are finite; a program needn't handle non-finite values.
Results may differ from a plain program's by a relative error of at most 0.02.
The roundings to bfloat16 on the way count: a program that leaves them out, or rounds other values in their place, can miss the bound.
Values may be sent and summed in bfloat16 or wider, within the bound.
A program may use at most 256 MiB of HBM per device.

v0:
```python
import jax
import jax.numpy as jnp
from jax import lax
from jax.sharding import PartitionSpec as P

P_SIZE = 64
N_STATE = 128
BLOCK_LEN = 256
E = 3072
norm_eps = 1e-05
beta_one = 0.9
beta_two = 0.95
adam_eps = 1e-08
adam_step = 3.0
weight_learning_rate = 0.01
matrix_decay = 0.1
small_rate = 0.1


def causal_conv(values, taps):
    length = values.shape[1]
    width = taps.shape[0] - 1
    padded = jnp.pad(values, ((0, 0), (width - 1, 0), (0, 0)))
    total = taps[width] + taps[0] * padded[:, 0:length]
    for shift in range(1, width):
        total = total + taps[shift] * padded[:, shift : shift + length]
    return total


def block_step(state, inputs):
    inner_part, step_part, learning_rate_piece, b_part, c_part = inputs
    high = lax.Precision.HIGHEST
    cumul = jnp.cumsum(learning_rate_piece, axis=1)
    scores = jnp.einsum("sin,sjn->sij", c_part, b_part, precision=high)
    rows = lax.broadcasted_iota(jnp.int32, (BLOCK_LEN, BLOCK_LEN), 0)
    cols = lax.broadcasted_iota(jnp.int32, (BLOCK_LEN, BLOCK_LEN), 1)
    lower = (rows >= cols)[None, :, :, None]
    spread = cumul[:, :, None, :] - cumul[:, None, :, :]
    decay = jnp.where(lower, jnp.exp(jnp.where(lower, spread, 0.0)), 0.0)
    weights = scores[..., None] * decay * step_part[:, None, :, :]
    within = jnp.einsum("sijh,sjhp->sihp", weights, inner_part, precision=high)
    carried = (
        jnp.einsum("sin,shpn->sihp", c_part, state, precision=high) * jnp.exp(cumul)[..., None]
    )
    tail = jnp.exp(cumul[:, -1:, :] - cumul) * step_part
    fresh = jnp.einsum("sjn,sjh,sjhp->shpn", b_part, tail, inner_part, precision=high)
    new_state = jnp.exp(cumul[:, -1, :])[:, :, None, None] * state + fresh
    return (new_state, within + carried)


def state_space(inner, step, rate, b_mat, c_mat):
    batch, length, heads, head_size = inner.shape
    blocks = length // BLOCK_LEN

    def blockify(values):
        return jnp.moveaxis(values.reshape((batch, blocks, BLOCK_LEN) + values.shape[2:]), 1, 0)

    start = jnp.zeros((batch, heads, head_size, b_mat.shape[2]), dtype=inner.dtype)
    _, outputs = lax.scan(
        jax.checkpoint(block_step),
        start,
        (blockify(inner), blockify(step), blockify(rate), blockify(b_mat), blockify(c_mat)),
    )
    return jnp.moveaxis(outputs, 0, 1).reshape(batch, length, heads, head_size)


def mixer(gate_inner, shared, step_raw, conv_local, conv_common, head_local):
    batch, length = (gate_inner.shape[0], gate_inner.shape[1])
    heads = step_raw.shape[2]
    parts = gate_inner.reshape(batch, length, heads, 2, P_SIZE)
    gate_vals = parts[:, :, :, 0, :].reshape(batch, length, heads * P_SIZE)
    inner_vals = parts[:, :, :, 1, :].reshape(batch, length, heads * P_SIZE)
    inner_act = jax.nn.silu(causal_conv(inner_vals, conv_local))
    shared_act = jax.nn.silu(causal_conv(shared, conv_common))
    half = shared.shape[2] // 2
    step = jax.nn.softplus(step_raw + head_local[0])
    rate = -step * jnp.exp(head_local[1])
    inner_heads = inner_act.reshape(batch, length, heads, P_SIZE)
    output = state_space(inner_heads, step, rate, shared_act[..., :half], shared_act[..., half:])
    output = output + head_local[2][:, None] * inner_heads
    return output.reshape(batch, length, heads * P_SIZE) * jax.nn.silu(gate_vals)


def adamw(param, grad, first, second_moment, rate, decay):
    first_new = beta_one * first + (1.0 - beta_one) * grad
    second_new = beta_two * second_moment + (1.0 - beta_two) * grad * grad
    corrected = (
        first_new
        / (1.0 - beta_one**adam_step)
        / (jnp.sqrt(second_new / (1.0 - beta_two**adam_step)) + adam_eps)
    )
    return (param - rate * (corrected + decay * param), first_new, second_new)


def local(
    block_in,
    cotangent,
    in_weight,
    out_weight,
    in_gain,
    out_gain,
    conv_inner,
    conv_shared,
    head_params,
    first_in_weight,
    first_out_weight,
    first_in_gain,
    first_out_gain,
    first_conv_inner,
    first_conv_shared,
    first_head_params,
    second_in_weight,
    second_out_weight,
    second_in_gain,
    second_out_gain,
    second_conv_inner,
    second_conv_shared,
    second_head_params,
):
    seq_index = lax.axis_index("seq")
    inputs = block_in.astype(jnp.float32)
    rms_in = lax.rsqrt(jnp.mean(inputs * inputs, axis=-1, keepdims=True) + norm_eps)
    normed = (inputs * rms_in * in_gain).astype(jnp.bfloat16)
    in_w16 = in_weight.astype(jnp.bfloat16)
    out_w16 = out_weight.astype(jnp.bfloat16)
    column_list = normed
    projected = jnp.einsum(
        "fbe,ek->fbk",
        column_list,
        lax.all_gather(in_w16, ("seq", "wshard"), axis=0, tiled=True),
        preferred_element_type=jnp.float32,
    ).astype(jnp.bfloat16)
    gate_inner = projected[:, :, : 2 * E]
    shared = projected[:, :, 2 * E : 2 * E + 2 * N_STATE]
    step_raw = projected[:, :, 2 * E + 2 * N_STATE :]
    head_gate, head_step = (
        lax.all_to_all(gate_inner, "seq", split_axis=2, concat_axis=1, tiled=True),
        lax.all_to_all(step_raw, "seq", split_axis=2, concat_axis=1, tiled=True),
    )
    head_shared = lax.all_gather(shared, "seq", axis=1, tiled=True)
    heads_dev = head_step.shape[2]
    inner_start = seq_index * (heads_dev * P_SIZE)
    conv_local = lax.dynamic_slice_in_dim(conv_inner, inner_start, heads_dev * P_SIZE, 1)
    head_local = lax.dynamic_slice_in_dim(head_params, seq_index * heads_dev, heads_dev, 1)
    gated, mixer_back = jax.vjp(
        mixer,
        head_gate.astype(jnp.float32),
        head_shared.astype(jnp.float32),
        head_step.astype(jnp.float32),
        conv_local,
        conv_shared,
        head_local,
    )
    gated32 = lax.all_to_all(
        gated.astype(jnp.bfloat16), "seq", split_axis=1, concat_axis=2, tiled=True
    ).astype(jnp.float32)
    rms_out = lax.rsqrt(jnp.mean(gated32 * gated32, axis=-1, keepdims=True) + norm_eps)
    gnormed = (gated32 * rms_out * out_gain).astype(jnp.bfloat16)
    column_list = gnormed
    mixed = jnp.einsum(
        "brg,ga->bra",
        column_list,
        lax.all_gather(out_w16, ("seq", "wshard"), axis=0, tiled=True),
        preferred_element_type=jnp.float32,
    )
    d_gnormed = jnp.einsum(
        "oum,am->oua",
        cotangent,
        lax.all_gather(out_w16, ("seq", "wshard"), axis=0, tiled=True),
        preferred_element_type=jnp.float32,
    )
    block_out = inputs + mixed
    d_out_gain = jnp.sum(d_gnormed * gated32 * rms_out, axis=(0, 1))
    scaled = d_gnormed * out_gain
    d_gated = (
        rms_out * scaled - gated32 * rms_out**3 * jnp.mean(scaled * gated32, axis=-1, keepdims=True)
    ).astype(jnp.bfloat16)
    head_cotan = lax.all_to_all(d_gated, "seq", split_axis=2, concat_axis=1, tiled=True).astype(
        jnp.float32
    )
    d_gate, d_shared, d_step, d_conv_local, d_common, d_head_local = mixer_back(head_cotan)
    tok_gate, tok_step = (
        lax.all_to_all(d_gate.astype(jnp.bfloat16), "seq", split_axis=1, concat_axis=2, tiled=True),
        lax.all_to_all(d_step.astype(jnp.bfloat16), "seq", split_axis=1, concat_axis=2, tiled=True),
    )
    shared_sum = lax.psum_scatter(
        d_shared.astype(jnp.bfloat16), "seq", scatter_dimension=1, tiled=True
    )
    projected_gradient = jnp.concatenate([tok_gate, shared_sum, tok_step], axis=2)
    d_normed = jnp.einsum(
        "ozu,hu->ozh",
        projected_gradient,
        lax.all_gather(in_w16, ("seq", "wshard"), axis=0, tiled=True),
        preferred_element_type=jnp.float32,
    )
    d_in_gain = jnp.sum(d_normed * inputs * rms_in, axis=(0, 1))
    scaled_in = d_normed * in_gain
    grad_in = (
        cotangent.astype(jnp.float32)
        + rms_in * scaled_in
        - inputs * rms_in**3 * jnp.mean(scaled_in * inputs, axis=-1, keepdims=True)
    )
    d_conv_full = lax.dynamic_update_slice_in_dim(
        jnp.zeros_like(conv_inner), d_conv_local, inner_start, 1
    )
    d_head_full = lax.dynamic_update_slice_in_dim(
        jnp.zeros_like(head_params), d_head_local, seq_index * heads_dev, 1
    )
    grad_in_gain, grad_out_gain, grad_conv_inner, grad_conv_shared, grad_head_params = lax.psum(
        (d_in_gain, d_out_gain, d_conv_full, d_common, d_head_full), ("seq", "wshard")
    )
    column_list = normed
    grad_in_weight = lax.psum_scatter(
        jnp.einsum(
            "nkm,nkc->mc", column_list, projected_gradient, preferred_element_type=jnp.float32
        ),
        ("seq", "wshard"),
        scatter_dimension=0,
        tiled=True,
    )
    column_list = gnormed
    grad_out_weight = lax.psum_scatter(
        jnp.einsum("kcb,kch->bh", column_list, cotangent, preferred_element_type=jnp.float32),
        ("seq", "wshard"),
        scatter_dimension=0,
        tiled=True,
    )
    new_in_weight, new_first_in_weight, new_second_in_weight = adamw(
        in_weight,
        grad_in_weight,
        first_in_weight,
        second_in_weight,
        weight_learning_rate,
        matrix_decay,
    )
    new_out_weight, new_first_out_weight, new_second_out_weight = adamw(
        out_weight,
        grad_out_weight,
        first_out_weight,
        second_out_weight,
        weight_learning_rate,
        matrix_decay,
    )
    updated_input_gain, new_first_in_gain, new_second_in_gain = adamw(
        in_gain, grad_in_gain, first_in_gain, second_in_gain, small_rate, 0.0
    )
    new_out_gain, new_first_out_gain, new_second_out_gain = adamw(
        out_gain, grad_out_gain, first_out_gain, second_out_gain, small_rate, 0.0
    )
    new_conv_inner, new_first_conv_inner, new_second_conv_inner = adamw(
        conv_inner, grad_conv_inner, first_conv_inner, second_conv_inner, small_rate, 0.0
    )
    new_conv_shared, new_first_conv_shared, new_second_conv_shared = adamw(
        conv_shared, grad_conv_shared, first_conv_shared, second_conv_shared, small_rate, 0.0
    )
    new_head_params, updated_head_first_moment, head_second_all = adamw(
        head_params, grad_head_params, first_head_params, second_head_params, small_rate, 0.0
    )
    return (
        block_out,
        grad_in,
        grad_in_weight,
        grad_out_weight,
        grad_in_gain,
        grad_out_gain,
        grad_conv_inner,
        grad_conv_shared,
        grad_head_params,
        new_in_weight,
        new_out_weight,
        updated_input_gain,
        new_out_gain,
        new_conv_inner,
        new_conv_shared,
        new_head_params,
        new_first_in_weight,
        new_first_out_weight,
        new_first_in_gain,
        new_first_out_gain,
        new_first_conv_inner,
        new_first_conv_shared,
        updated_head_first_moment,
        new_second_in_weight,
        new_second_out_weight,
        new_second_in_gain,
        new_second_out_gain,
        new_second_conv_inner,
        new_second_conv_shared,
        head_second_all[0:2],
        head_second_all[2],
    )


def solution(mesh):
    return jax.shard_map(
        local,
        mesh=mesh,
        in_specs=(
            P("wshard", "seq", None),
            P("wshard", "seq", None),
            P(("seq", "wshard"), None),
            P(("seq", "wshard"), None),
            P(),
            P(),
            P(),
            P(),
            P(),
            P(("seq", "wshard"), None),
            P(("seq", "wshard"), None),
            P(),
            P(),
            P(),
            P(),
            P(),
            P(("seq", "wshard"), None),
            P(("seq", "wshard"), None),
            P(),
            P(),
            P(),
            P(),
            P(),
        ),
        out_specs=(
            P("wshard", "seq", None),
            P("wshard", "seq", None),
            P(("seq", "wshard"), None),
            P(("seq", "wshard"), None),
            P(),
            P(),
            P(),
            P(),
            P(),
            P(("seq", "wshard"), None),
            P(("seq", "wshard"), None),
            P(),
            P(),
            P(),
            P(),
            P(),
            P(("seq", "wshard"), None),
            P(("seq", "wshard"), None),
            P(),
            P(),
            P(),
            P(),
            P(),
            P(("seq", "wshard"), None),
            P(("seq", "wshard"), None),
            P(),
            P(),
            P(),
            P(),
            P(),
            P(),
        ),
        check_vma=False,
    )
```

profile of v0, /device:TPU:0, one launch (start us, length us, event | category | flops | bytes accessed | tf_op | source)
XLA Modules:
  0.0 2023.6 jit_solution(13329375079531035761)
XLA Ops:
  11.6 132.1 %all-gather.4.cloned.1.call-done = bf16[1536,6448]{1,0:T(8,128)(2,1)} async-done(((bf16[48,6448]{1,0:T(8,128)(2,1)}), bf16[1536,6448]{1,0:T(8,128)(2,1)}) %all-gather.4.cloned.1.call-update) | async-done | bytes 19808272 | tf_op jit(solution)/shard_map/all_gather | solution.py:130
  143.6 14.0 fusion.107
  167.6 37.2 %copy.613 = bf16[1,256,6144]{1,0,2:T(2,128)(2,1)} copy(bf16[1,256,6144]{1,2,0:T(8,128)(2,1)S(1)} %slice.200) | data formatting | bytes 6291456 | tf_op jit(solution)/shard_map/slice | solution.py:133
  204.9 31.5 %reduce.89 = bf16[6144,256]{1,0:T(8,128)(2,1)S(1)} reduce(bf16[6144,1,256]{2,1,0:T(2,128)(2,1)} %bitcast.657, bf16[]{:T(256)} %broadcast.1020), dimensions={1}, to_apply=%bitcast.470.reduce_sub_computation | reduce | bytes 6291458
  259.4 23.1 %all-to-all-done.1 = bf16[8,2,98304]{2,1,0:T(2,128)(2,1)S(1)} async-done(((bf16[8,2,98304]{2,1,0:T(2,128)(2,1)}), bf16[8,2,98304]{2,1,0:T(2,128)(2,1)S(1)}, u32[]{:S(2)}, u32[]{:S(2)}) %all-to-all-start.1) | async-done | bytes 3145760 | tf_op jit(solution)/shard_map/all_to_all | solution.py:137
  317.7 185.0 %while.44 = (s32[]{:T(128)}, f32[1,6,64,128]{3,2,1,0:T(8,128)S(1)}, f32[8,1,256,6,64]{2,0,4,3,1:T(8,128)}, f32[8,1,6,64,128]{4,3,2,1,0:T(8,128)}, f32[8,1,256,6]...) while((s32[]{:T(128)}, f32[1,6,64,128]{3,2,1,0:T(8,128)S(1)}, ...), condition=%wide.region_4.5_spmd.clone.clone, body=%wide.region_1.4_spmd.clone.clone.sunk | while | flops 707349504 | bytes 5805416 | solution.py:59
  331.4 9.8 dynamic_update_slice.95
  520.5 35.5 %reduce.90 = bf16[2048,384]{1,0:T(8,128)(2,1)} reduce(bf16[2048,1,384]{2,1,0:T(2,128)(2,1)} %bitcast.669, bf16[]{:T(256)} %broadcast.1020), dimensions={1}, to_apply=%bitcast.432.reduce_sub_computation | reduce | bytes 3145730
  564.1 20.9 %all-to-all-done.2 = bf16[8,2,49152]{2,1,0:T(2,128)(2,1)} async-done(((bf16[8,2,49152]{2,1,0:T(2,128)(2,1)}), bf16[8,2,49152]{2,1,0:T(2,128)(2,1)}, u32[]{:S(2)}, u32[]{:S(2)}) %all-to-all-start.2) | async-done | bytes 1572896 | tf_op jit(solution)/shard_map/all_to_all | solution.py:154
  600.2 10.7 fusion.139
  610.9 204.3 %reduce-scatter.8.cloned.1.call-done = f32[96,1536]{1,0:T(8,128)} async-done(((f32[3072,1536]{1,0:T(8,128)}), f32[96,1536]{1,0:T(8,128)}) %reduce-scatter.8.cloned.1.call-update) | async-done | bytes 589840 | tf_op jit(solution)/shard_map/reduce_scatter | solution.py:222
  822.5 76.8 %all-gather.8.cloned.1.call-done = bf16[3072,1536]{1,0:T(8,128)(2,1)} async-done(((bf16[96,1536]{1,0:T(8,128)(2,1)}), bf16[3072,1536]{1,0:T(8,128)(2,1)}) %all-gather.8.cloned.1.call-update) | async-done | bytes 9437200 | tf_op jit(solution)/shard_map/all_gather | solution.py:163
  917.6 17.8 reduce.91
  947.2 17.2 all-to-all-done.3
  981.4 355.6 %while.43 = (s32[]{:T(128)}, f32[1,6,64,128]{3,2,1,0:T(8,128)S(1)}, f32[8,1,256,6,64]{2,0,4,3,1:T(8,128)}, f32[8,1,256,6]{3,2,1,0:T(8,128)}, f32[8,1,256,6]{2,0,...) while((s32[]{:T(128)}, f32[1,6,64,128]{3,2,1,0:T(8,128)S(1)}, ...), condition=%wide.region_19.20_spmd.clone, body=%wide.region_7.19_spmd.clone.sunk | while | flops 1670419456 | bytes 15714059 | solution.py:59
  1341.8 11.5 reduce.92
  1369.0 12.4 multiply_reduce_fusion.6
  1392.1 15.7 copy.509
  1407.8 31.6 %reduce.93 = bf16[2048,768]{1,0:T(8,128)(2,1)S(1)} reduce(bf16[2048,1,768]{2,1,0:T(2,128)(2,1)} %bitcast.656, bf16[]{:T(256)} %broadcast.1020), dimensions={1}, to_apply=%bitcast.438.reduce_sub_computation | reduce | bytes 6291458
  1460.7 27.7 %all-to-all-done.4 = bf16[8,2,98304]{2,1,0:T(2,128)(2,1)} async-done(((bf16[8,2,98304]{2,1,0:T(2,128)(2,1)}), bf16[8,2,98304]{2,1,0:T(2,128)(2,1)}, u32[]{:S(2)}, u32[]{:S(2)}) %all-to-all-start.4) | async-done | bytes 3145760 | tf_op jit(solution)/shard_map/all_to_all | solution.py:183
  1502.4 12.5 fusion.132
  1515.0 18.5 fusion.135
  1545.1 94.3 %all-reduce.32.cloned.1.call-done = (f32[1536]{0:T(1024)}, f32[3072]{0:T(1024)}, f32[5,3072]{1,0:T(8,128)}, f32[5,256]{1,0:T(8,128)}, f32[3,48]{1,0:T(4,128)}) async-done(((f32[1536]{0:T(1024)}, f32[3072]{0:T(1024)}, f32[5,3072]{1,0:T(8,128)}, f32[5,256]{1,0:T(8,128)}, f32[3,48]{1,0:T(4,128)}), (f32[1536]{0:T(1024)}, f32[3072]{0:T(1024)}, f32[5,3072]{1,0:T(8,128)}, f32[5,256]{1,0:T(8,128)}, ...) | async-done | bytes 85584 | tf_op jit(solution)/shard_map/psum | solution.py:209
  1647.4 361.7 %reduce-scatter.6.cloned.1.call-done = f32[48,6448]{1,0:T(8,128)} async-done(((f32[1536,6448]{1,0:T(8,128)}), f32[48,6448]{1,0:T(8,128)}) %reduce-scatter.6.cloned.1.call-update) | async-done | bytes 1238032 | tf_op jit(solution)/shard_map/reduce_scatter | solution.py:213
  (963 shorter events, 787.9 us)
Async XLA Ops:
  7.2 136.4 %all-gather.4.cloned.1.call-start = ((), (), s32[]{:S(2)}) async-start(), calls=%async_computation.9 | async-start | bytes 20680704 | tf_op jit(solution)/shard_map/all_gather | solution.py:130
  9.6 238.6 %all-gather.6.cloned.1.call-start = ((), (), s32[]{:S(2)}) async-start(), calls=%async_computation.10 | async-start | bytes 1179648 | tf_op jit(solution)/shard_map/all_gather | solution.py:140
  11.6 146.1 %copy-start.48 = (f32[256]{0:T(256)}, f32[256]{0:T(256)S(1)}, u32[]{:S(2)}) copy-start(f32[256]{0:T(256)S(1)} %get-tuple-element.934) | copy-start | bytes 3076
  162.0 78.0 %all-to-all-start = ((bf16[8,2,768]{2,1,0:T(2,128)(2,1)}), bf16[8,2,768]{2,1,0:T(2,128)(2,1)S(1)}, u32[]{:S(2)}, u32[]{:S(2)}) async-start(bf16[8,2,768]{2,1,0:T(2,128)(2,1)} %reshape.1691), calls=%async_computation | async-start | bytes 49152 | tf_op jit(solution)/shard_map/all_to_all | solution.py:138
  240.0 42.4 %all-to-all-start.1 = ((bf16[8,2,98304]{2,1,0:T(2,128)(2,1)}), bf16[8,2,98304]{2,1,0:T(2,128)(2,1)S(1)}, u32[]{:S(2)}, u32[]{:S(2)}) async-start(bf16[8,2,98304]{2,1,0:T(2,128)(2,1)} %reshape.1693), calls=%async_computation.1 | async-start | bytes 6291456 | tf_op jit(solution)/shard_map/all_to_all | solution.py:137
  244.9 262.4 %copy-start.46 = (f32[384]{0:T(512)}, f32[384]{0:T(512)S(1)}, u32[]{:S(2)}) copy-start(f32[384]{0:T(512)S(1)} %mul.1143) | copy-start | bytes 4612
  307.2 636.9 %copy-start = (f32[1,2048,6,1,64]{1,4,3,2,0:T(8,128)}, f32[1,2048,6,1,64]{1,4,3,2,0:T(8,128)S(1)}, u32[]{:S(2)}) copy-start(f32[1,2048,6,1,64]{1,4,3,2,0:T(8,128)S(1)} %get-tuple-element.912) | copy-start | bytes 9437188
  559.7 25.3 %all-to-all-start.2 = ((bf16[8,2,49152]{2,1,0:T(2,128)(2,1)}), bf16[8,2,49152]{2,1,0:T(2,128)(2,1)}, u32[]{:S(2)}, u32[]{:S(2)}) async-start(bf16[8,2,49152]{2,1,0:T(2,128)(2,1)} %reshape.1695), calls=%async_computation.2 | async-start | bytes 3145728 | tf_op jit(solution)/shard_map/all_to_all | solution.py:154
  564.1 251.1 %reduce-scatter.8.cloned.1.call-start = ((), (), s32[]{:S(2)}) async-start(), calls=%async_computation.14 | async-start | bytes 19464192 | tf_op jit(solution)/shard_map/reduce_scatter | solution.py:222
  595.9 311.8 %copy-start.60 = (f32[256]{0:T(256)}, f32[256]{0:T(256)S(1)}, u32[]{:S(2)}) copy-start(f32[256]{0:T(256)S(1)} %get-tuple-element.936) | copy-start | bytes 3076
  610.9 288.4 %all-gather.8.cloned.1.call-start = ((), (), s32[]{:S(2)}) async-start(), calls=%async_computation.11 | async-start | bytes 9732096 | tf_op jit(solution)/shard_map/all_gather | solution.py:163
  939.1 25.3 %all-to-all-start.3 = ((bf16[8,2,49152]{2,1,0:T(2,128)(2,1)}), bf16[8,2,49152]{2,1,0:T(2,128)(2,1)}, u32[]{:S(2)}, u32[]{:S(2)}) async-start(bf16[8,2,49152]{2,1,0:T(2,128)(2,1)} %reshape.1697), calls=%async_computation.3 | async-start | bytes 3145728 | tf_op jit(solution)/shard_map/all_to_all | solution.py:178
  1354.7 88.3 %all-to-all-start.5 = ((bf16[8,2,768]{2,1,0:T(2,128)(2,1)}), bf16[8,2,768]{2,1,0:T(2,128)(2,1)S(1)}, u32[]{:S(2)}, u32[]{:S(2)}) async-start(bf16[8,2,768]{2,1,0:T(2,128)(2,1)} %reshape.1699), calls=%async_computation.6 | async-start | bytes 49152 | tf_op jit(solution)/shard_map/all_to_all | solution.py:184
  1443.0 45.4 %all-to-all-start.4 = ((bf16[8,2,98304]{2,1,0:T(2,128)(2,1)}), bf16[8,2,98304]{2,1,0:T(2,128)(2,1)}, u32[]{:S(2)}, u32[]{:S(2)}) async-start(bf16[8,2,98304]{2,1,0:T(2,128)(2,1)} %reshape.1701), calls=%async_computation.4 | async-start | bytes 6291456 | tf_op jit(solution)/shard_map/all_to_all | solution.py:183
  1447.7 54.6 %reduce-scatter.4.cloned.1.call-start = ((), (), s32[]{:S(2)}) async-start(), calls=%async_computation.12 | async-start | bytes 1179648 | tf_op jit(solution)/shard_map/reduce_scatter | solution.py:186
  1455.5 184.0 %all-reduce.32.cloned.1.call-start = ((), (), s32[]{:S(2)}) async-start(), calls=%async_computation.15 | async-start | bytes 258048 | tf_op jit(solution)/shard_map/psum | solution.py:209
  1514.9 494.2 %reduce-scatter.6.cloned.1.call-start = ((), (), s32[]{:S(2)}) async-start(), calls=%async_computation.13 | async-start | bytes 41361408 | tf_op jit(solution)/shard_map/reduce_scatter | solution.py:213
  1543.4 465.7 %copy-start.13 = (f32[48,6448]{1,0:T(8,128)S(1)}, f32[48,6448]{1,0:T(8,128)}, u32[]{:S(2)}) copy-start(f32[48,6448]{1,0:T(8,128)} %param.29) | copy-start | bytes 3714052
  1543.4 465.7 %copy-start.18 = (f32[48,6448]{1,0:T(8,128)S(1)}, f32[48,6448]{1,0:T(8,128)}, u32[]{:S(2)}) copy-start(f32[48,6448]{1,0:T(8,128)} %param.36) | copy-start | bytes 3714052
  1647.4 365.9 %copy-start.35 = (f32[1536]{0:T(1024)S(1)}, f32[1536]{0:T(1024)}, u32[]{:S(2)}) copy-start(f32[1536]{0:T(1024)} %get-tuple-element.1242) | copy-start | bytes 18436
  1647.4 366.5 %copy-start.33 = (f32[3072]{0:T(1024)S(1)}, f32[3072]{0:T(1024)}, u32[]{:S(2)}) copy-start(f32[3072]{0:T(1024)} %get-tuple-element.1243) | copy-start | bytes 36868
  1647.4 367.1 %copy-start.21 = (f32[5,3072]{1,0:T(8,128)S(1)}, f32[5,3072]{1,0:T(8,128)}, u32[]{:S(2)}) copy-start(f32[5,3072]{1,0:T(8,128)} %get-tuple-element.1244) | copy-start | bytes 184324
  1647.4 367.8 %copy-start.34 = (f32[5,256]{1,0:T(8,128)S(1)}, f32[5,256]{1,0:T(8,128)}, u32[]{:S(2)}) copy-start(f32[5,256]{1,0:T(8,128)} %get-tuple-element.1245) | copy-start | bytes 15364
  1647.4 368.4 %copy-start.73 = (f32[3,48]{1,0:T(4,128)S(1)}, f32[3,48]{1,0:T(4,128)}, u32[]{:S(2)}) copy-start(f32[3,48]{1,0:T(4,128)} %get-tuple-element.1246) | copy-start | bytes 1732
  (96 other events, 2495.9 us)
Sparse Core Ops, SparseCore 0:
  11.4 132.1 all-gather.3
  159.4 21.6 all-gather.5
  611.0 204.1 reduce-scatter.7
  818.7 80.5 all-gather.7
  1455.6 38.7 reduce-scatter.3
  1515.0 124.3 all-reduce.31
  1646.4 362.6 reduce-scatter.5
where the time goes:
time: 2040 us; the launch traced here: 2020 us
  waiting for transfers between devices  958 us (47%)
  local copies, waits for them, and re-layouts  484 us (24%)
  other arithmetic  326 us (16%)
  matrix products  211 us (10%)
  starting transfers between devices  25.1 us (1%)
    reduce_scatter x1, waiting for transfers between devices, local(): lax.psum_scatter(jnp.einsum('nkm,nkc->mc', column_list, projected_gradien...  362 us
    dynamic_update_slice x56, local copies, waits for them, and re-layouts, state_space(): lax.scan(jax.checkpoint(block_step), start, (blockify(inner), blockify(st...  215 us
    reduce_scatter x1, waiting for transfers between devices, local(): lax.psum_scatter(jnp.einsum('kcb,kch->bh', column_list, cotangent, prefer...  204 us
    all_gather x1, waiting for transfers between devices, local(): lax.all_gather(in_w16, ('seq', 'wshard'), axis=0, tiled=True)  132 us
    unnamed x10, other arithmetic  132 us
    psum x1, waiting for transfers between devices, local(): lax.psum((d_in_gain, d_out_gain, d_conv_full, d_common, d_head_full), ('s...  94.3 us
    another operation x49, other arithmetic  93.2 us
    all_gather x1, waiting for transfers between devices, local(): lax.all_gather(out_w16, ('seq', 'wshard'), axis=0, tiled=True)  76.8 us
  transfers between devices with their start and end apart: 13, of which 9 were waited for; matrix products, arithmetic and copies ran while one was open for 12% of the time, Pallas kernels for 0%

commit v1 on v0

--- a/solution.py
+++ b/solution.py
@@ -127,7 +127,12 @@
     projected = jnp.einsum(
         "fbe,ek->fbk",
         column_list,
-        lax.all_gather(in_w16, ("seq", "wshard"), axis=0, tiled=True),
+        jnp.concatenate(
+            lax.all_to_all(
+                jnp.stack([in_w16] * lax.axis_size(("seq", "wshard"))), ("seq", "wshard"), 0, 0
+            ),
+            axis=0,
+        ),
         preferred_element_type=jnp.float32,
     ).astype(jnp.bfloat16)
     gate_inner = projected[:, :, : 2 * E]

time: 2040 us -> 2450 us (1.20)
  waiting for transfers between devices: 958 us -> 1270 us
  matrix products: 211 us -> 252 us
  local copies, waits for them, and re-layouts: 484 us -> 520 us
    all_to_all x0 -> x1, waiting for transfers between devices: none -> 430 us  [local(): lax.all_to_all(jnp.stack([in_w16] * lax.axis_size(('seq', 'wshard'))), ('...]
    all_gather x1, waiting for transfers between devices: 132 us -> 0.01 us  [local(): lax.all_gather(in_w16, ('seq', 'wshard'), axis=0, tiled=True)]
    unnamed x177 -> x183, local copies, waits for them, and re-layouts: 69 us -> 73.3 us
  transfers between devices with their start and end apart: 13 -> 14, of which waited for: 9 -> 9; matrix products, arithmetic and copies ran while one was open for 12% -> 29% of each run, Pallas kernels for 0% -> 0%
where the time goes in v1:
time: 2450 us; the launch traced here: 2440 us
  waiting for transfers between devices  1270 us (52%)
  local copies, waits for them, and re-layouts  520 us (21%)
  other arithmetic  341 us (14%)
  matrix products  252 us (10%)
  starting transfers between devices  33.5 us (1%)
    all_to_all x1, waiting for transfers between devices, local(): lax.all_to_all(jnp.stack([in_w16] * lax.axis_size(('seq', 'wshard'))), ('...  430 us
    reduce_scatter x1, waiting for transfers between devices, local(): lax.psum_scatter(jnp.einsum('nkm,nkc->mc', column_list, projected_gradien...  362 us
    reduce_scatter x1, waiting for transfers between devices, local(): lax.psum_scatter(jnp.einsum('kcb,kch->bh', column_list, cotangent, prefer...  218 us
    dynamic_update_slice x56, local copies, waits for them, and re-layouts, state_space(): lax.scan(jax.checkpoint(block_step), start, (blockify(inner), blockify(st...  215 us
    unnamed x10, other arithmetic  134 us
    psum x1, waiting for transfers between devices, local(): lax.psum((d_in_gain, d_out_gain, d_conv_full, d_common, d_head_full), ('s...  94.2 us
    another operation x49, other arithmetic  93.2 us
    dot_general x24, matrix products, block_step(): within = jnp.einsum('sijh,sjhp->sihp', weights, inner_part, precision=high)  83.5 us
  transfers between devices with their start and end apart: 14, of which 9 were waited for; matrix products, arithmetic and copies ran while one was open for 29% of the time, Pallas kernels for 0%

profile of v1, /device:TPU:0, one launch (start us, length us, event | category | flops | bytes accessed | tf_op | source)
XLA Modules:
  0.0 2438.2 jit_solution(497407998636934374)
XLA Ops:
  24.7 429.7 %all-to-all-done = bf16[32,48,6448]{2,1,0:T(8,128)(2,1)} async-done(((bf16[32,48,6448]{2,1,0:T(8,128)(2,1)}), bf16[32,48,6448]{2,1,0:T(8,128)(2,1)}, u32[]{:S(2)}, u32[]{:S(2)}) %all-to-all-start) | async-done | bytes 19808288 | tf_op jit(solution)/shard_map/all_to_all | solution.py:131
  454.5 14.0 fusion.107
  479.5 37.2 %copy.613 = bf16[1,256,6144]{1,0,2:T(2,128)(2,1)} copy(bf16[1,256,6144]{1,2,0:T(8,128)(2,1)S(1)} %slice.200) | data formatting | bytes 6291456 | tf_op jit(solution)/shard_map/slice | solution.py:138
  516.7 31.6 %reduce.89 = bf16[6144,256]{1,0:T(8,128)(2,1)S(1)} reduce(bf16[6144,1,256]{2,1,0:T(2,128)(2,1)} %bitcast.658, bf16[]{:T(256)} %broadcast.1022), dimensions={1}, to_apply=%bitcast.471.reduce_sub_computation | reduce | bytes 6291458
  571.3 23.1 all-to-all-done.2
  629.6 192.2 %while.44 = (s32[]{:T(128)}, f32[1,6,64,128]{3,2,1,0:T(8,128)S(1)}, f32[8,1,256,6,64]{2,0,4,3,1:T(8,128)}, f32[8,1,6,64,128]{4,3,2,1,0:T(8,128)}, f32[8,1,256,6]...) while((s32[]{:T(128)}, f32[1,6,64,128]{3,2,1,0:T(8,128)S(1)}, ...), condition=%wide.region_4.5_spmd.clone.clone, body=%wide.region_1.4_spmd.clone.clone.sunk | while | flops 707349504 | bytes 5806421 | solution.py:59
  839.6 35.5 %reduce.90 = bf16[2048,384]{1,0:T(8,128)(2,1)} reduce(bf16[2048,1,384]{2,1,0:T(2,128)(2,1)} %bitcast.670, bf16[]{:T(256)} %broadcast.1022), dimensions={1}, to_apply=%bitcast.433.reduce_sub_computation | reduce | bytes 3145730
  883.2 20.9 all-to-all-done.3
  919.3 10.7 fusion.139
  930.0 217.9 %reduce-scatter.8.cloned.1.call-done = f32[96,1536]{1,0:T(8,128)} async-done(((f32[3072,1536]{1,0:T(8,128)}), f32[96,1536]{1,0:T(8,128)}) %reduce-scatter.8.cloned.1.call-update) | async-done | bytes 589840 | tf_op jit(solution)/shard_map/reduce_scatter | solution.py:227
  1155.2 76.8 %all-gather.6.cloned.1.call-done = bf16[3072,1536]{1,0:T(8,128)(2,1)} async-done(((bf16[96,1536]{1,0:T(8,128)(2,1)}), bf16[3072,1536]{1,0:T(8,128)(2,1)}) %all-gather.6.cloned.1.call-update) | async-done | bytes 9437200 | tf_op jit(solution)/shard_map/all_gather | solution.py:168
  1250.3 17.8 reduce.91
  1280.5 21.1 all-to-all-done.4
  1320.8 433.8 %while.43 = (s32[]{:T(128)}, f32[1,6,64,128]{3,2,1,0:T(8,128)S(1)}, f32[8,1,256,6,64]{2,0,4,3,1:T(8,128)}, f32[8,1,256,6]{3,2,1,0:T(8,128)}, f32[8,1,256,6]{2,0,...) while((s32[]{:T(128)}, f32[1,6,64,128]{3,2,1,0:T(8,128)S(1)}, ...), condition=%wide.region_19.20_spmd.clone, body=%wide.region_7.19_spmd.clone.sunk | while | flops 1670419456 | bytes 15190127 | solution.py:59
  1364.9 9.8 dynamic_update_slice.91
  1770.7 13.4 reduce.92
  1790.1 12.1 multiply_reduce_fusion.6
  1806.4 11.3 copy.509
  1817.7 31.7 %reduce.93 = bf16[2048,768]{1,0:T(8,128)(2,1)S(1)} reduce(bf16[2048,1,768]{2,1,0:T(2,128)(2,1)} %bitcast.657, bf16[]{:T(256)} %broadcast.1022), dimensions={1}, to_apply=%bitcast.439.reduce_sub_computation | reduce | bytes 6291458
  1875.4 27.8 %all-to-all-done.5 = bf16[8,2,98304]{2,1,0:T(2,128)(2,1)} async-done(((bf16[8,2,98304]{2,1,0:T(2,128)(2,1)}), bf16[8,2,98304]{2,1,0:T(2,128)(2,1)}, u32[]{:S(2)}, u32[]{:S(2)}) %all-to-all-start.5) | async-done | bytes 3145760 | tf_op jit(solution)/shard_map/all_to_all | solution.py:188
  1917.2 12.5 fusion.132
  1929.8 18.6 fusion.135
  1960.0 94.2 %all-reduce.32.cloned.1.call-done = (f32[1536]{0:T(1024)}, f32[3072]{0:T(1024)}, f32[5,3072]{1,0:T(8,128)}, f32[5,256]{1,0:T(8,128)}, f32[3,48]{1,0:T(4,128)}) async-done(((f32[1536]{0:T(1024)}, f32[3072]{0:T(1024)}, f32[5,3072]{1,0:T(8,128)}, f32[5,256]{1,0:T(8,128)}, f32[3,48]{1,0:T(4,128)}), (f32[1536]{0:T(1024)}, f32[3072]{0:T(1024)}, f32[5,3072]{1,0:T(8,128)}, f32[5,256]{1,0:T(8,128)}, ...) | async-done | bytes 85584 | tf_op jit(solution)/shard_map/psum | solution.py:214
  2062.2 361.7 %reduce-scatter.6.cloned.1.call-done = f32[48,6448]{1,0:T(8,128)} async-done(((f32[1536,6448]{1,0:T(8,128)}), f32[48,6448]{1,0:T(8,128)}) %reduce-scatter.6.cloned.1.call-update) | async-done | bytes 1238032 | tf_op jit(solution)/shard_map/reduce_scatter | solution.py:218
  (956 shorter events, 890.8 us)
Async XLA Ops:
  16.4 438.1 %copy-start.28 = (f32[1536]{0:T(1024)S(1)}, f32[1536]{0:T(1024)}, u32[]{:S(2)}) copy-start(f32[1536]{0:T(1024)} %param.31) | copy-start | bytes 18436
  16.4 438.1 %all-to-all-start = ((bf16[32,48,6448]{2,1,0:T(8,128)(2,1)}), bf16[32,48,6448]{2,1,0:T(8,128)(2,1)}, u32[]{:S(2)}, u32[]{:S(2)}) async-start(bf16[32,48,6448]{2,1,0:T(8,128)(2,1)} %stack.2), calls=%async_computation | async-start | bytes 40108032 | tf_op jit(solution)/shard_map/all_to_all | solution.py:131
  23.9 536.2 %all-gather.4.cloned.1.call-start = ((), (), s32[]{:S(2)}) async-start(), calls=%async_computation.10 | async-start | bytes 1179648 | tf_op jit(solution)/shard_map/all_gather | solution.py:145
  24.7 443.8 %copy-start.50 = (f32[256]{0:T(256)}, f32[256]{0:T(256)S(1)}, u32[]{:S(2)}) copy-start(f32[256]{0:T(256)S(1)} %get-tuple-element.934) | copy-start | bytes 3076
  473.0 78.9 %all-to-all-start.1 = ((bf16[8,2,768]{2,1,0:T(2,128)(2,1)}), bf16[8,2,768]{2,1,0:T(2,128)(2,1)S(1)}, u32[]{:S(2)}, u32[]{:S(2)}) async-start(bf16[8,2,768]{2,1,0:T(2,128)(2,1)} %reshape.1697), calls=%async_computation.1 | async-start | bytes 49152 | tf_op jit(solution)/shard_map/all_to_all | solution.py:143
  551.9 42.4 %all-to-all-start.2 = ((bf16[8,2,98304]{2,1,0:T(2,128)(2,1)}), bf16[8,2,98304]{2,1,0:T(2,128)(2,1)S(1)}, u32[]{:S(2)}, u32[]{:S(2)}) async-start(bf16[8,2,98304]{2,1,0:T(2,128)(2,1)} %reshape.1699), calls=%async_computation.2 | async-start | bytes 6291456 | tf_op jit(solution)/shard_map/all_to_all | solution.py:142
  558.5 718.2 %copy-start.19 = (bf16[48,1,256]{2,1,0:T(2,128)(2,1)}, bf16[48,1,256]{2,1,0:T(2,128)(2,1)S(1)}, u32[]{:S(2)}) copy-start(bf16[48,1,256]{2,1,0:T(2,128)(2,1)S(1)} %reshape.1698) | copy-start | bytes 73732
  619.1 658.3 %copy-start = (f32[1,2048,6,1,64]{1,4,3,2,0:T(8,128)}, f32[1,2048,6,1,64]{1,4,3,2,0:T(8,128)S(1)}, u32[]{:S(2)}) copy-start(f32[1,2048,6,1,64]{1,4,3,2,0:T(8,128)S(1)} %get-tuple-element.912) | copy-start | bytes 9437188
  878.9 25.3 %all-to-all-start.3 = ((bf16[8,2,49152]{2,1,0:T(2,128)(2,1)}), bf16[8,2,49152]{2,1,0:T(2,128)(2,1)}, u32[]{:S(2)}, u32[]{:S(2)}) async-start(bf16[8,2,49152]{2,1,0:T(2,128)(2,1)} %reshape.1701), calls=%async_computation.3 | async-start | bytes 3145728 | tf_op jit(solution)/shard_map/all_to_all | solution.py:159
  883.2 264.7 %reduce-scatter.8.cloned.1.call-start = ((), (), s32[]{:S(2)}) async-start(), calls=%async_computation.15 | async-start | bytes 19464192 | tf_op jit(solution)/shard_map/reduce_scatter | solution.py:227
  930.0 302.0 %all-gather.6.cloned.1.call-start = ((), (), s32[]{:S(2)}) async-start(), calls=%async_computation.11 | async-start | bytes 9732096 | tf_op jit(solution)/shard_map/all_gather | solution.py:168
  1271.8 29.8 %all-to-all-start.4 = ((bf16[8,2,49152]{2,1,0:T(2,128)(2,1)}), bf16[8,2,49152]{2,1,0:T(2,128)(2,1)}, u32[]{:S(2)}, u32[]{:S(2)}) async-start(bf16[8,2,49152]{2,1,0:T(2,128)(2,1)} %reshape.1703), calls=%async_computation.4 | async-start | bytes 3145728 | tf_op jit(solution)/shard_map/all_to_all | solution.py:183
  1276.1 641.1 %all-gather.8.cloned.1.call-start = ((), (), s32[]{:S(2)}) async-start(), calls=%async_computation.13 | async-start | bytes 20680704 | tf_op jit(solution)/shard_map/all_gather | solution.py:198
  1786.5 71.3 %all-to-all-start.6 = ((bf16[8,2,768]{2,1,0:T(2,128)(2,1)}), bf16[8,2,768]{2,1,0:T(2,128)(2,1)S(1)}, u32[]{:S(2)}, u32[]{:S(2)}) async-start(bf16[8,2,768]{2,1,0:T(2,128)(2,1)} %reshape.1705), calls=%async_computation.7 | async-start | bytes 49152 | tf_op jit(solution)/shard_map/all_to_all | solution.py:189
  1857.8 45.4 %all-to-all-start.5 = ((bf16[8,2,98304]{2,1,0:T(2,128)(2,1)}), bf16[8,2,98304]{2,1,0:T(2,128)(2,1)}, u32[]{:S(2)}, u32[]{:S(2)}) async-start(bf16[8,2,98304]{2,1,0:T(2,128)(2,1)} %reshape.1707), calls=%async_computation.5 | async-start | bytes 6291456 | tf_op jit(solution)/shard_map/all_to_all | solution.py:188
  1862.5 54.7 %reduce-scatter.4.cloned.1.call-start = ((), (), s32[]{:S(2)}) async-start(), calls=%async_computation.12 | async-start | bytes 1179648 | tf_op jit(solution)/shard_map/reduce_scatter | solution.py:191
  1870.2 184.0 %all-reduce.32.cloned.1.call-start = ((), (), s32[]{:S(2)}) async-start(), calls=%async_computation.16 | async-start | bytes 258048 | tf_op jit(solution)/shard_map/psum | solution.py:214
  1929.7 494.1 %reduce-scatter.6.cloned.1.call-start = ((), (), s32[]{:S(2)}) async-start(), calls=%async_computation.14 | async-start | bytes 41361408 | tf_op jit(solution)/shard_map/reduce_scatter | solution.py:218
  1958.3 465.6 %copy-start.13 = (f32[48,6448]{1,0:T(8,128)S(1)}, f32[48,6448]{1,0:T(8,128)}, u32[]{:S(2)}) copy-start(f32[48,6448]{1,0:T(8,128)} %param.29) | copy-start | bytes 3714052
  1958.3 465.6 %copy-start.18 = (f32[48,6448]{1,0:T(8,128)S(1)}, f32[48,6448]{1,0:T(8,128)}, u32[]{:S(2)}) copy-start(f32[48,6448]{1,0:T(8,128)} %param.36) | copy-start | bytes 3714052
  2062.2 366.5 %copy-start.35 = (f32[3072]{0:T(1024)S(1)}, f32[3072]{0:T(1024)}, u32[]{:S(2)}) copy-start(f32[3072]{0:T(1024)} %get-tuple-element.1243) | copy-start | bytes 36868
  2062.2 367.1 %copy-start.23 = (f32[5,3072]{1,0:T(8,128)S(1)}, f32[5,3072]{1,0:T(8,128)}, u32[]{:S(2)}) copy-start(f32[5,3072]{1,0:T(8,128)} %get-tuple-element.1244) | copy-start | bytes 184324
  2062.2 367.7 %copy-start.36 = (f32[5,256]{1,0:T(8,128)S(1)}, f32[5,256]{1,0:T(8,128)}, u32[]{:S(2)}) copy-start(f32[5,256]{1,0:T(8,128)} %get-tuple-element.1245) | copy-start | bytes 15364
  2062.2 368.3 %copy-start.75 = (f32[3,48]{1,0:T(4,128)S(1)}, f32[3,48]{1,0:T(4,128)}, u32[]{:S(2)}) copy-start(f32[3,48]{1,0:T(4,128)} %get-tuple-element.1246) | copy-start | bytes 1732
  (92 other events, 2958.8 us)
Sparse Core Ops, SparseCore 0:
  470.3 36.6 all-gather.3
  930.1 217.7 reduce-scatter.7
  1151.4 80.5 all-gather.5
  1279.4 132.7 all-gather.7
  1870.3 38.6 reduce-scatter.3
  1929.9 124.2 all-reduce.31
  2061.2 362.6 reduce-scatter.5
